TPU v7x, 32 devices: a whole 2x2x4 slice. The times are simulated.
32 devices in a mesh: rep: 8 (over y, x, core), fsdp: 4 (over z).
Axes of the slice: x: 2, y: 2, z: 4, core: 2. Of those that a mesh axis runs over, the one named last changes fastest.
Arguments:
- tokens: bfloat16 [16384, 768], P(('rep', 'fsdp')), may hold values from -6 to 6
- cotangent: bfloat16 [16384, 768], P(('rep', 'fsdp')), may hold values from -6 to 6
- lengths: int32 [32], P(('rep', 'fsdp')), may hold values from 1 to 512, 10240 in all
- slot_seq: int32 [32], replicated, may hold values from 0 to 31, each once
- query_weight: bfloat16 [768, 768], P('fsdp'), may hold values from -0.21875 to 0.21875
- query_bias: bfloat16 [768], P('fsdp'), may hold values from -2 to 2
- key_weight: bfloat16 [768, 768], P('fsdp'), may hold values from -0.21875 to 0.21875
- value_weight: bfloat16 [768, 768], P('fsdp'), may hold values from -0.21875 to 0.21875
- value_bias: bfloat16 [768], P('fsdp'), may hold values from -2 to 2
- out_weight: bfloat16 [768, 768], P('fsdp'), may hold values from -2.5 to 2.5
- out_bias: bfloat16 [768], P('fsdp'), may hold values from -2 to 2
- first_gain: bfloat16 [768], P('fsdp'), may hold values from 0.5 to 1.5
- first_shift: bfloat16 [768], P('fsdp'), may hold values from -2 to 2
- inner_weight: bfloat16 [768, 3072], P('fsdp'), may hold values from -0.21875 to 0.21875
- inner_bias: bfloat16 [3072], P('fsdp'), may hold values from -2 to 2
- outer_weight: bfloat16 [3072, 768], P('fsdp'), may hold values from -0.109375 to 0.109375
- outer_bias: bfloat16 [768], P('fsdp'), may hold values from -2 to 2
- second_gain: bfloat16 [768], P('fsdp'), may hold values from 0.5 to 1.5
- second_shift: bfloat16 [768], P('fsdp'), may hold values from -2 to 2
Outputs:
- output: bfloat16 [16384, 768], P(('rep', 'fsdp'))
- grad_tokens: bfloat16 [16384, 768], P(('rep', 'fsdp'))
- query_weight_grad: float32 [768, 768], P('fsdp')
- query_bias_grad: float32 [768], P('fsdp')
- key_weight_grad: float32 [768, 768], P('fsdp')
- value_weight_grad: float32 [768, 768], P('fsdp')
- value_bias_grad: float32 [768], P('fsdp')
- out_weight_grad: float32 [768, 768], P('fsdp')
- out_bias_grad: float32 [768], P('fsdp')
- first_gain_grad: float32 [768], P('fsdp')
- first_shift_grad: float32 [768], P('fsdp')
- inner_weight_grad: float32 [768, 3072], P('fsdp')
- inner_bias_grad: float32 [3072], P('fsdp')
- outer_weight_grad: float32 [3072, 768], P('fsdp')
- outer_bias_grad: float32 [768], P('fsdp')
- second_gain_grad: float32 [768], P('fsdp')
- second_shift_grad: float32 [768], P('fsdp')
Inputs may be any that keep to these rules, and one draw needn't show every extreme that they name: Every sequence has at least one token; the longest has exactly 512; the lengths add up to 10240. `slot_seq`: each sequence fills exactly one slot.
All inputs are finite; a program needn't handle non-finite values. No bound on the sum of `lengths` on one device may be relied on, other than what follows from the above.
Results may differ from a plain program's by a relative error of at most 0.017.
Values may be sent and summed in bfloat16 or wider, within the bound.
A program may use at most 128 MiB of HBM per device.

v0:
```python
import math
import jax
import jax.numpy as jnp
from jax import lax
from jax.sharding import PartitionSpec as P

HEADS = 12
HD = 64
norm_eps = 1e-12
masked_score = -1e30
inv_root_two = 0.7071067811865476
inv_root_two_pi = 0.3989422804014327


def matmul(left, right):
    return jnp.dot(left, right, preferred_element_type=jnp.float32)


def matmul_left_t(left, right):
    return lax.dot_general(
        left, right, (((0,), (0,)), ((), ())), preferred_element_type=jnp.float32
    )


def matmul_right_t(left, right):
    return lax.dot_general(
        left, right, (((1,), (1,)), ((), ())), preferred_element_type=jnp.float32
    )


def norm_forward(values, norm_gain, norm_shift):
    center = values - jnp.mean(values, axis=-1, keepdims=True)
    spread = jnp.mean(center * center, axis=-1, keepdims=True)
    scaled_inv = lax.rsqrt(spread + norm_eps)
    normed = center * scaled_inv
    return (normed * norm_gain + norm_shift, normed, scaled_inv)


def norm_backward(grad_out, normed, scaled_inv, norm_gain):
    grad_normed = grad_out * norm_gain
    first_mean = jnp.mean(grad_normed, axis=-1, keepdims=True)
    second_mean = jnp.mean(grad_normed * normed, axis=-1, keepdims=True)
    return (grad_normed - first_mean - normed * second_mean) * scaled_inv


def score_block(query_block, key_rows, kept_keys):
    scores = jnp.einsum(
        "qhd,khd->hqk", query_block, key_rows, preferred_element_type=jnp.float32
    ) * HD ** (-0.5)
    return jnp.where(kept_keys[None, None, :], scores, masked_score)


def attention_forward(query_rows, key_rows, value_rows, kept_keys, block_rows):
    seq_len = query_rows.shape[0]

    def one_block(query_block):
        scores = score_block(query_block, key_rows, kept_keys)
        largest = jnp.max(scores, axis=-1, keepdims=True)
        weights = jnp.exp(scores - largest)
        row_total = jnp.sum(weights, axis=-1, keepdims=True)
        chances = (weights / row_total).astype(jnp.bfloat16)
        context = jnp.einsum(
            "hqk,khd->qhd", chances, value_rows, preferred_element_type=jnp.float32
        )
        return (context, largest + jnp.log(row_total))

    blocks = query_rows.reshape(seq_len // block_rows, block_rows, HEADS, HD)
    context, log_total = lax.map(one_block, blocks)
    return (context.reshape(seq_len, HEADS * HD), log_total)


def attention_backward(
    query_rows, key_rows, value_rows, kept_keys, grad_context, log_total, block_rows
):
    seq_len = query_rows.shape[0]
    block_count = seq_len // block_rows
    scale = HD ** (-0.5)

    def one_block(carry, item):
        grad_keys, grad_values = carry
        query_block, grad_block, log_block = item
        scores = score_block(query_block, key_rows, kept_keys)
        chances = jnp.exp(scores - log_block)
        grad_chances = jnp.einsum(
            "qhd,khd->hqk", grad_block, value_rows, preferred_element_type=jnp.float32
        )
        centered = jnp.sum(chances * grad_chances, axis=-1, keepdims=True)
        grad_scores = (chances * (grad_chances - centered)).astype(jnp.bfloat16)
        grad_query = (
            jnp.einsum("hqk,khd->qhd", grad_scores, key_rows, preferred_element_type=jnp.float32)
            * scale
        )
        grad_keys = (
            grad_keys
            + jnp.einsum(
                "hqk,qhd->khd", grad_scores, query_block, preferred_element_type=jnp.float32
            )
            * scale
        )
        grad_values = grad_values + jnp.einsum(
            "hqk,qhd->khd",
            chances.astype(jnp.bfloat16),
            grad_block,
            preferred_element_type=jnp.float32,
        )
        return ((grad_keys, grad_values), grad_query)

    start = jnp.zeros(key_rows.shape, jnp.float32)
    items = (
        query_rows.reshape(block_count, block_rows, HEADS, HD),
        grad_context.reshape(block_count, block_rows, HEADS, HD),
        log_total,
    )
    (grad_keys, grad_values), grad_query = lax.scan(one_block, (start, start), items)
    return (
        grad_query.reshape(seq_len, HEADS * HD),
        grad_keys.reshape(seq_len, HEADS * HD),
        grad_values.reshape(seq_len, HEADS * HD),
    )


def shards(
    tokens,
    cotangent,
    lengths,
    slot_seq,
    query_weight,
    query_bias,
    key_weight,
    value_weight,
    value_bias,
    out_weight,
    out_bias,
    first_gain,
    first_shift,
    inner_weight,
    inner_bias,
    outer_weight,
    outer_bias,
    second_gain,
    second_shift,
):
    peer_count = lax.axis_size(("rep", "fsdp"))
    row_count, feature_dim = tokens.shape
    piece_rows = row_count // peer_count
    slots = jnp.arange(peer_count, dtype=jnp.int32)
    inverse = jnp.sum(jnp.where(slot_seq[None, :] == slots[:, None], slots[None, :], 0), axis=1)

    def outgoing(array):
        return jnp.take(
            array.reshape(peer_count, piece_rows, feature_dim), inverse, axis=0
        ).reshape(row_count, feature_dim)

    def incoming(array):
        return jnp.take(
            array.reshape(peer_count, piece_rows, feature_dim), slot_seq, axis=0
        ).reshape(row_count, feature_dim)

    seq_rows, seq_seed = (
        lax.all_to_all(outgoing(tokens), ("rep", "fsdp"), split_axis=0, concat_axis=0, tiled=True),
        lax.all_to_all(
            outgoing(cotangent), ("rep", "fsdp"), split_axis=0, concat_axis=0, tiled=True
        ),
    )
    kept = jnp.arange(row_count, dtype=jnp.int32) < lengths[0]
    (
        query_full,
        query_bias_full,
        key_full,
        value_full,
        value_bias_full,
        out_full,
        out_bias_full,
        first_gain_full,
        first_shift_full,
        inner_full,
        inner_bias_full,
        outer_full,
        outer_bias_full,
        second_gain_full,
        second_shift_full,
    ) = (
        lax.all_gather(query_weight, "fsdp", axis=0, tiled=True),
        lax.all_gather(query_bias, "fsdp", axis=0, tiled=True),
        lax.all_gather(key_weight, "fsdp", axis=0, tiled=True),
        lax.all_gather(value_weight, "fsdp", axis=0, tiled=True),
        lax.all_gather(value_bias, "fsdp", axis=0, tiled=True),
        lax.all_gather(out_weight, "fsdp", axis=0, tiled=True),
        lax.all_gather(out_bias, "fsdp", axis=0, tiled=True),
        lax.all_gather(first_gain, "fsdp", axis=0, tiled=True),
        lax.all_gather(first_shift, "fsdp", axis=0, tiled=True),
        lax.all_gather(inner_weight, "fsdp", axis=0, tiled=True),
        lax.all_gather(inner_bias, "fsdp", axis=0, tiled=True),
        lax.all_gather(outer_weight, "fsdp", axis=0, tiled=True),
        lax.all_gather(outer_bias, "fsdp", axis=0, tiled=True),
        lax.all_gather(second_gain, "fsdp", axis=0, tiled=True),
        lax.all_gather(second_shift, "fsdp", axis=0, tiled=True),
    )
    block_rows = math.gcd(row_count, 512)
    head_shape = (row_count, HEADS, HD)
    query_rows = (
        (matmul(seq_rows, query_full) + query_bias_full.astype(jnp.float32))
        .astype(jnp.bfloat16)
        .reshape(head_shape)
    )
    key_rows = matmul(seq_rows, key_full).astype(jnp.bfloat16).reshape(head_shape)
    value_rows = (
        (matmul(seq_rows, value_full) + value_bias_full.astype(jnp.float32))
        .astype(jnp.bfloat16)
        .reshape(head_shape)
    )
    context, log_total = attention_forward(query_rows, key_rows, value_rows, kept, block_rows)
    context = context.astype(jnp.bfloat16)
    attended = matmul(context, out_full) + out_bias_full.astype(jnp.float32)
    hidden, first_normed, first_inv = norm_forward(
        seq_rows.astype(jnp.float32) + attended,
        first_gain_full.astype(jnp.float32),
        first_shift_full.astype(jnp.float32),
    )
    hidden_low = hidden.astype(jnp.bfloat16)
    inner = matmul(hidden_low, inner_full) + inner_bias_full.astype(jnp.float32)
    activated = jax.nn.gelu(inner, approximate=False).astype(jnp.bfloat16)
    outer = matmul(activated, outer_full) + outer_bias_full.astype(jnp.float32)
    result, second_normed, second_inv = norm_forward(
        hidden + outer, second_gain_full.astype(jnp.float32), second_shift_full.astype(jnp.float32)
    )
    result = jnp.where(kept[:, None], result, 0.0).astype(jnp.bfloat16)
    (
        query_back,
        key_back,
        value_back,
        out_back,
        first_gain_back,
        inner_back,
        outer_back,
        second_gain_back,
    ) = (
        lax.all_gather(query_weight, "fsdp", axis=0, tiled=True),
        lax.all_gather(key_weight, "fsdp", axis=0, tiled=True),
        lax.all_gather(value_weight, "fsdp", axis=0, tiled=True),
        lax.all_gather(out_weight, "fsdp", axis=0, tiled=True),
        lax.all_gather(first_gain, "fsdp", axis=0, tiled=True),
        lax.all_gather(inner_weight, "fsdp", axis=0, tiled=True),
        lax.all_gather(outer_weight, "fsdp", axis=0, tiled=True),
        lax.all_gather(second_gain, "fsdp", axis=0, tiled=True),
    )
    seed_rows = jnp.where(kept[:, None], seq_seed.astype(jnp.float32), 0.0)
    grad_second_gain = jnp.sum(seed_rows * second_normed, axis=0)
    grad_second_shift = jnp.sum(seed_rows, axis=0)
    grad_second = norm_backward(
        seed_rows, second_normed, second_inv, second_gain_back.astype(jnp.float32)
    )
    grad_outer = grad_second.astype(jnp.bfloat16)
    grad_outer_bias = jnp.sum(grad_outer, axis=0, dtype=jnp.float32)
    grad_outer_weight = matmul_left_t(activated, grad_outer)
    grad_activated = matmul_right_t(grad_outer, outer_back)
    slope = (
        0.5 * (1.0 + lax.erf(inner * inv_root_two))
        + inner * jnp.exp(-0.5 * inner * inner) * inv_root_two_pi
    )
    grad_inner = (grad_activated * slope).astype(jnp.bfloat16)
    grad_inner_bias = jnp.sum(grad_inner, axis=0, dtype=jnp.float32)
    grad_inner_weight = matmul_left_t(hidden_low, grad_inner)
    grad_hidden = grad_second + matmul_right_t(grad_inner, inner_back)
    grad_first_gain = jnp.sum(grad_hidden * first_normed, axis=0)
    grad_first_shift = jnp.sum(grad_hidden, axis=0)
    grad_residual = norm_backward(
        grad_hidden, first_normed, first_inv, first_gain_back.astype(jnp.float32)
    )
    grad_attended = grad_residual.astype(jnp.bfloat16)
    grad_out_bias = jnp.sum(grad_attended, axis=0, dtype=jnp.float32)
    grad_out_weight = matmul_left_t(context, grad_attended)
    grad_context = matmul_right_t(grad_attended, out_back).astype(jnp.bfloat16)
    grad_query, grad_key, grad_value = attention_backward(
        query_rows,
        key_rows,
        value_rows,
        kept,
        grad_context.reshape(head_shape),
        log_total,
        block_rows,
    )
    grad_query = grad_query.astype(jnp.bfloat16)
    grad_key = grad_key.astype(jnp.bfloat16)
    grad_value = grad_value.astype(jnp.bfloat16)
    grad_query_bias = jnp.sum(grad_query, axis=0, dtype=jnp.float32)
    grad_value_bias = jnp.sum(grad_value, axis=0, dtype=jnp.float32)
    grad_query_weight = matmul_left_t(seq_rows, grad_query)
    grad_key_weight = matmul_left_t(seq_rows, grad_key)
    grad_value_weight = matmul_left_t(seq_rows, grad_value)
    grad_input = (
        grad_residual
        + matmul_right_t(grad_query, query_back)
        + matmul_right_t(grad_key, key_back)
        + matmul_right_t(grad_value, value_back)
    ).astype(jnp.bfloat16)
    shares = (
        lax.psum_scatter(
            grad_query_weight.astype(jnp.bfloat16), "fsdp", scatter_dimension=0, tiled=True
        ).astype(jnp.float32),
        lax.psum_scatter(
            grad_query_bias.astype(jnp.bfloat16), "fsdp", scatter_dimension=0, tiled=True
        ).astype(jnp.float32),
        lax.psum_scatter(
            grad_key_weight.astype(jnp.bfloat16), "fsdp", scatter_dimension=0, tiled=True
        ).astype(jnp.float32),
        lax.psum_scatter(
            grad_value_weight.astype(jnp.bfloat16), "fsdp", scatter_dimension=0, tiled=True
        ).astype(jnp.float32),
        lax.psum_scatter(
            grad_value_bias.astype(jnp.bfloat16), "fsdp", scatter_dimension=0, tiled=True
        ).astype(jnp.float32),
        lax.psum_scatter(
            grad_out_weight.astype(jnp.bfloat16), "fsdp", scatter_dimension=0, tiled=True
        ).astype(jnp.float32),
        lax.psum_scatter(
            grad_out_bias.astype(jnp.bfloat16), "fsdp", scatter_dimension=0, tiled=True
        ).astype(jnp.float32),
        lax.psum_scatter(
            grad_first_gain.astype(jnp.bfloat16), "fsdp", scatter_dimension=0, tiled=True
        ).astype(jnp.float32),
        lax.psum_scatter(
            grad_first_shift.astype(jnp.bfloat16), "fsdp", scatter_dimension=0, tiled=True
        ).astype(jnp.float32),
        lax.psum_scatter(
            grad_inner_weight.astype(jnp.bfloat16), "fsdp", scatter_dimension=0, tiled=True
        ).astype(jnp.float32),
        lax.psum_scatter(
            grad_inner_bias.astype(jnp.bfloat16), "fsdp", scatter_dimension=0, tiled=True
        ).astype(jnp.float32),
        lax.psum_scatter(
            grad_outer_weight.astype(jnp.bfloat16), "fsdp", scatter_dimension=0, tiled=True
        ).astype(jnp.float32),
        lax.psum_scatter(
            grad_outer_bias.astype(jnp.bfloat16), "fsdp", scatter_dimension=0, tiled=True
        ).astype(jnp.float32),
        lax.psum_scatter(
            grad_second_gain.astype(jnp.bfloat16), "fsdp", scatter_dimension=0, tiled=True
        ).astype(jnp.float32),
        lax.psum_scatter(
            grad_second_shift.astype(jnp.bfloat16), "fsdp", scatter_dimension=0, tiled=True
        ).astype(jnp.float32),
    )
    totals = lax.psum(tuple(shares), "rep")
    back_rows, back_grads = (
        lax.all_to_all(result, ("rep", "fsdp"), split_axis=0, concat_axis=0, tiled=True),
        lax.all_to_all(grad_input, ("rep", "fsdp"), split_axis=0, concat_axis=0, tiled=True),
    )
    return (incoming(back_rows), incoming(back_grads)) + tuple(totals)


def solution(mesh):
    placed = (
        P(("rep", "fsdp"), None),
        P(("rep", "fsdp"), None),
        P(("rep", "fsdp")),
        P(),
        P("fsdp", None),
        P("fsdp"),
        P("fsdp", None),
        P("fsdp", None),
        P("fsdp"),
        P("fsdp", None),
        P("fsdp"),
        P("fsdp"),
        P("fsdp"),
        P("fsdp", None),
        P("fsdp"),
        P("fsdp", None),
        P("fsdp"),
        P("fsdp"),
        P("fsdp"),
    )
    return jax.shard_map(
        shards,
        mesh=mesh,
        in_specs=placed,
        out_specs=(
            P(("rep", "fsdp"), None),
            P(("rep", "fsdp"), None),
            P("fsdp", None),
            P("fsdp"),
            P("fsdp", None),
            P("fsdp", None),
            P("fsdp"),
            P("fsdp", None),
            P("fsdp"),
            P("fsdp"),
            P("fsdp"),
            P("fsdp", None),
            P("fsdp"),
            P("fsdp", None),
            P("fsdp"),
            P("fsdp"),
            P("fsdp"),
        ),
        check_vma=False,
    )
```

profile of v0, /device:TPU:0, one launch (start us, length us, event | category | flops | bytes accessed | tf_op | source)
XLA Modules:
  0.0 826.6 jit_solution(8898270440098371738)
XLA Ops:
  13.2 44.4 %all_to_all.33 = bf16[32,16,768]{2,1,0:T(8,128)(2,1)S(1)} all-to-all(bf16[32,16,768]{2,1,0:T(8,128)(2,1)S(1)} %get-tuple-element.117), channel_id=1, replica_groups=mesh['rep'=8,'fsdp'=4] {'rep','fsdp'}, dimensions={0} | all-to-all | bytes 1572864 | tf_op jit(solution)/shard_map/all_to_all | solution.py:161
  57.5 3.8 all-to-all-start
  65.5 40.4 %all-reduce.19 = (bf16[768]{0:T(1024)(128)(2,1)S(1)}, bf16[768]{0:T(1024)(128)(2,1)S(1)}, bf16[768]{0:T(1024)(128)(2,1)S(1)}, bf16[768]{0:T(1024)(128)(2,1)S(1)}...) all-reduce(bf16[768]{0:T(1024)(128)(2,1)S(1)} %dynamic-update-slice, ...), channel_id=1, replica_groups=mesh['rep'=8,'fsdp'=4] {'fsdp'}, use_global_device_ids=true, to_apply=%add | all-reduce | flops 5376 | bytes 21504
  106.0 14.0 %all-gather = bf16[4,1,768]{2,1,0:T(2,128)(2,1)S(1)} all-gather(bf16[1,1,768]{2,1,0:T(2,128)(2,1)S(1)} %reshape.251), channel_id=1, replica_groups=mesh['rep'=8,'fsdp'=4] {'fsdp'}, dimensions={0}, use_global_device_ids=true | all-gather | bytes 7680 | tf_op jit(solution)/shard_map/all_gather | solution.py:193
  120.6 2.3 add_convert_fusion.1
  123.2 3.2 convolution_convert_fusion.7
  126.4 1.4 copy.66
  127.8 3.0 fusion.37
  130.9 4.5 copy-done.2
  135.4 1.8 fusion
  137.2 2.9 add_convert_fusion.2
  140.1 1.4 copy.64
  141.6 8.0 fusion.27
  149.6 13.9 %all-gather.14.cloned.1.call-done = bf16[768,768]{1,0:T(8,128)(2,1)} async-done(((bf16[192,768]{1,0:T(8,128)(2,1)}), bf16[768,768]{1,0:T(8,128)(2,1)}) %all-gather.14.cloned.1.call-update) | async-done | bytes 1179664 | tf_op jit(solution)/shard_map/all_gather | solution.py:188
  163.5 2.7 fusion.38
  166.5 87.1 %all-gather.16.cloned.1.call-done = bf16[768,3072]{1,0:T(8,128)(2,1)} async-done(((bf16[192,3072]{1,0:T(8,128)(2,1)}), bf16[768,3072]{1,0:T(8,128)(2,1)}) %all-gather.16.cloned.1.call-update) | async-done | bytes 4718608 | tf_op jit(solution)/shard_map/all_gather | solution.py:192
  253.6 19.3 %fusion.4 = (bf16[512,3072]{1,0:T(8,128)(2,1)}, f32[512,3072]{1,0:T(8,128)}) fusion(f32[3072]{0:T(1024)S(1)} %bitcast.109, bf16[768,3072]{1,0:T(8,128)(2,1)} %all-gather.16.cloned.1.call-done, f32[512,768]{1,0:T(8,128)S(1)} %get-tuple-element.122, f32[768]{0:T(1024)S(1)} %convert_element_type.228, f32[768]{0:T(1024)S(1)} %convert_element_type.227, ...), kind=kOutput, calls=%fused_computation.16 | convolution fusion | flops 2521694208 | bytes 15751168 | tf_op jit(solution)/shard_map/dot_general | solution.py:16
  272.9 70.0 %all-gather.18.cloned.1.call-done = bf16[3072,768]{1,0:T(8,128)(2,1)} async-done(((bf16[768,768]{1,0:T(8,128)(2,1)}), bf16[3072,768]{1,0:T(8,128)(2,1)}) %all-gather.18.cloned.1.call-update) | async-done | bytes 4718608 | tf_op jit(solution)/shard_map/all_gather | solution.py:194
  342.9 6.6 fusion.39
  351.1 1.2 copy-done.27
  352.4 4.9 fusion.40
  357.4 3.1 multiply_reduce_fusion.2
  362.2 1.8 convolution_convert_fusion.2
  364.1 3.4 convolution_convert_fusion.6
  367.5 1.5 copy.68
  369.0 6.8 bitcast_reduce_fusion
  376.8 1.9 convolution_convert_fusion.3
  378.7 6.4 multiply_reduce_fusion
  385.1 6.9 multiply_convert_fusion
  392.0 1.2 bitcast_reduce_fusion.1
  393.2 1.5 copy-done.3
  395.5 1.9 convolution_convert_fusion.5
  397.7 5.0 multiply_convert_fusion.1
  403.6 1.9 convolution_convert_fusion.4
  405.6 7.2 convolution_convert_fusion
  412.8 7.4 convolution_convert_fusion.1
  421.3 16.8 %all-reduce.18 = (bf16[768]{0:T(1024)(128)(2,1)S(1)}, bf16[768]{0:T(1024)(128)(2,1)S(1)}, bf16[768]{0:T(1024)(128)(2,1)S(1)}, bf16[768]{0:T(1024)(128)(2,1)S(1)}...) all-reduce(bf16[768]{0:T(1024)(128)(2,1)S(1)} %dynamic-update-slice, ...), channel_id=1, replica_groups=mesh['rep'=8,'fsdp'=4] {'fsdp'}, use_global_device_ids=true, to_apply=%add.7 | all-reduce | flops 9984 | bytes 39936
  438.0 1.6 select_convert_fusion
  439.6 4.3 all-to-all-start.1
  445.2 2.2 fusion.41
  449.4 1.7 add_convert_fusion
  451.1 19.0 %all-to-all-done.1 = bf16[32,16,768]{2,1,0:T(8,128)(2,1)S(1)} async-done(((bf16[32,16,768]{2,1,0:T(8,128)(2,1)}), bf16[32,16,768]{2,1,0:T(8,128)(2,1)S(1)}, u32[]{:S(2)}, u32[]{:S(2)}) %all-to-all-start.1) | async-done | bytes 786464 | tf_op jit(solution)/shard_map/all_to_all | solution.py:346
  470.1 5.5 all-to-all-start.3
  476.9 26.4 %all-to-all-done.3 = bf16[32,16,768]{2,1,0:T(8,128)(2,1)S(1)} async-done(((bf16[32,16,768]{2,1,0:T(8,128)(2,1)}), bf16[32,16,768]{2,1,0:T(8,128)(2,1)S(1)}, u32[]{:S(2)}, u32[]{:S(2)}) %all-to-all-start.3) | async-done | bytes 786464 | tf_op jit(solution)/shard_map/all_to_all | solution.py:347
  503.9 1.3 broadcast_select_fusion
  505.3 81.5 %reduce-scatter.17.cloned.1.call-done = bf16[768,768]{1,0:T(8,128)(2,1)} async-done(((bf16[3072,768]{1,0:T(8,128)(2,1)}), bf16[768,768]{1,0:T(8,128)(2,1)}) %reduce-scatter.17.cloned.1.call-update) | async-done | bytes 1179664 | tf_op jit(solution)/shard_map/reduce_scatter | solution.py:331
  586.8 88.0 %reduce-scatter.15.cloned.1.call-done = bf16[192,3072]{1,0:T(8,128)(2,1)} async-done(((bf16[768,3072]{1,0:T(8,128)(2,1)}), bf16[192,3072]{1,0:T(8,128)(2,1)}) %reduce-scatter.15.cloned.1.call-update) | async-done | bytes 1179664 | tf_op jit(solution)/shard_map/reduce_scatter | solution.py:325
  674.7 144.6 %all-reduce.21 = (f32[192,768]{1,0:T(8,128)}, f32[192]{0:T(256)}, f32[192,768]{1,0:T(8,128)}, f32[192,768]{1,0:T(8,128)}, f32[192]{0:T(256)}, /*index=5*/f32[192...) all-reduce(bf16[192,768]{1,0:T(8,128)(2,1)} %reduce-scatter.7.clone, ...), channel_id=1, replica_groups=mesh['rep'=8,'fsdp'=4] {'rep'}, use_global_device_ids=true, to_apply=%region_13.15 | all-reduce | flops 1771776 | bytes 10635264 | tf_op jit(solution)/shard_map/psum | solution.py:344
  (185 shorter events, 21.3 us)
Async XLA Ops:
  7.2 3.6 copy-start
  7.2 3.4 copy-start.37
  7.2 4.2 copy-start.18
  7.2 113.3 %all-gather.10.cloned.1.call-start = ((), (), s32[]{:S(2)}) async-start(), calls=%async_computation.11 | async-start | bytes 1474560 | tf_op jit(solution)/shard_map/all_gather | solution.py:183
  8.0 115.2 %all-gather.12.cloned.1.call-start = ((), (), s32[]{:S(2)}) async-start(), calls=%async_computation.12 | async-start | bytes 1474560 | tf_op jit(solution)/shard_map/all_gather | solution.py:185
  8.7 128.5 %all-gather.8.cloned.1.call-start = ((), (), s32[]{:S(2)}) async-start(), calls=%async_computation.10 | async-start | bytes 1474560 | tf_op jit(solution)/shard_map/all_gather | solution.py:186
  9.4 154.1 %all-gather.14.cloned.1.call-start = ((), (), s32[]{:S(2)}) async-start(), calls=%async_computation.13 | async-start | bytes 1474560 | tf_op jit(solution)/shard_map/all_gather | solution.py:188
  10.0 243.6 %all-gather.16.cloned.1.call-start = ((), (), s32[]{:S(2)}) async-start(), calls=%async_computation.14 | async-start | bytes 5898240 | tf_op jit(solution)/shard_map/all_gather | solution.py:192
  13.1 49.5 %copy-start.25 = (u32[32]{0:T(128)S(1)}, u32[32]{0:T(128)}, u32[]{:S(2)}) copy-start(u32[32]{0:T(128)} %constant.140) | copy-start | bytes 388
  13.1 50.8 %copy-start.29 = (bf16[192]{0:T(256)(128)(2,1)S(1)}, bf16[192]{0:T(256)(128)(2,1)}, u32[]{:S(2)}) copy-start(bf16[192]{0:T(256)(128)(2,1)} %param.38) | copy-start | bytes 1156
  13.1 51.0 %copy-start.30 = (bf16[192]{0:T(256)(128)(2,1)S(1)}, bf16[192]{0:T(256)(128)(2,1)}, u32[]{:S(2)}) copy-start(bf16[192]{0:T(256)(128)(2,1)} %param.37) | copy-start | bytes 1156
  13.1 51.3 %copy-start.31 = (bf16[192]{0:T(256)(128)(2,1)S(1)}, bf16[192]{0:T(256)(128)(2,1)}, u32[]{:S(2)}) copy-start(bf16[192]{0:T(256)(128)(2,1)} %param.32) | copy-start | bytes 1156
  13.1 51.5 %copy-start.32 = (bf16[192]{0:T(256)(128)(2,1)S(1)}, bf16[192]{0:T(256)(128)(2,1)}, u32[]{:S(2)}) copy-start(bf16[192]{0:T(256)(128)(2,1)} %param.33) | copy-start | bytes 1156
  13.1 51.7 %copy-start.33 = (bf16[192]{0:T(256)(128)(2,1)S(1)}, bf16[192]{0:T(256)(128)(2,1)}, u32[]{:S(2)}) copy-start(bf16[192]{0:T(256)(128)(2,1)} %param.31) | copy-start | bytes 1156
  13.1 52.0 %copy-start.34 = (bf16[192]{0:T(256)(128)(2,1)S(1)}, bf16[192]{0:T(256)(128)(2,1)}, u32[]{:S(2)}) copy-start(bf16[192]{0:T(256)(128)(2,1)} %param.26) | copy-start | bytes 1156
  13.1 52.2 %copy-start.35 = (bf16[192]{0:T(256)(128)(2,1)S(1)}, bf16[192]{0:T(256)(128)(2,1)}, u32[]{:S(2)}) copy-start(bf16[192]{0:T(256)(128)(2,1)} %param.29) | copy-start | bytes 1156
  13.1 92.8 %copy-start.26 = (bf16[768]{0:T(1024)(128)(2,1)S(1)}, bf16[768]{0:T(1024)(128)(2,1)}, u32[]{:S(2)}) copy-start(bf16[768]{0:T(1024)(128)(2,1)} %param.35) | copy-start | bytes 4612
  57.5 63.0 %all-to-all-start = ((bf16[32,16,768]{2,1,0:T(8,128)(2,1)}), bf16[32,16,768]{2,1,0:T(8,128)(2,1)S(1)}, u32[]{:S(2)}, u32[]{:S(2)}) async-start(bf16[32,16,768]{2,1,0:T(8,128)(2,1)} %get-tuple-element.118), calls=%async_computation | async-start | bytes 1572864 | tf_op jit(solution)/shard_map/all_to_all | solution.py:160
  61.3 281.5 %all-gather.18.cloned.1.call-start = ((), (), s32[]{:S(2)}) async-start(), calls=%async_computation.15 | async-start | bytes 5898240 | tf_op jit(solution)/shard_map/all_gather | solution.py:194
  61.9 443.3 %reduce-scatter.13.cloned.1.call-start = ((), (), s32[]{:S(2)}) async-start(), calls=%async_computation.19 | async-start | bytes 1474560 | tf_op jit(solution)/shard_map/reduce_scatter | solution.py:313
  120.5 16.7 %copy-start.19 = (bf16[32,16,768]{2,1,0:T(8,128)(2,1)}, bf16[32,16,768]{2,1,0:T(8,128)(2,1)S(1)}, u32[]{:S(2)}) copy-start(bf16[32,16,768]{2,1,0:T(8,128)(2,1)S(1)} %all-to-all-done) | copy-start | bytes 2359300
  123.2 4.7 copy-start.6
  130.9 4.5 copy-start.2
  141.6 8.0 copy-start.10
  166.2 106.7 %copy-start.8 = (f32[512,768]{1,0:T(8,128)}, f32[512,768]{1,0:T(8,128)S(1)}, u32[]{:S(2)}) copy-start(f32[512,768]{1,0:T(8,128)S(1)} %get-tuple-element.122) | copy-start | bytes 4718596
  342.9 8.3 %copy-start.40 = (f32[512,3072]{1,0:T(8,128)S(1)}, f32[512,3072]{1,0:T(8,128)}, u32[]{:S(2)}) copy-start(f32[512,3072]{1,0:T(8,128)} %get-tuple-element.124) | copy-start | bytes 18874372
  349.8 2.6 copy-start.27
  350.5 6.8 slice-start
  351.1 6.2 copy-start.15
  352.4 5.0 copy-start.9
  352.4 5.0 slice-start.1
  357.3 3.2 copy-start.39
  364.0 141.2 %reduce-scatter.11.cloned.1.call-start = ((), (), s32[]{:S(2)}) async-start(), calls=%async_computation.18 | async-start | bytes 1474560 | tf_op jit(solution)/shard_map/reduce_scatter | solution.py:307
  369.0 7.7 copy-start.20
  378.7 126.6 %reduce-scatter.7.cloned.1.call-start = ((), (), s32[]{:S(2)}) async-start(), calls=%async_computation.16 | async-start | bytes 1474560 | tf_op jit(solution)/shard_map/reduce_scatter | solution.py:298
  392.0 2.7 copy-start.3
  392.0 3.5 copy-start.21
  394.7 3.1 copy-start.7
  397.4 6.2 copy-start.22
  397.4 107.9 %reduce-scatter.9.cloned.1.call-start = ((), (), s32[]{:S(2)}) async-start(), calls=%async_computation.17 | async-start | bytes 1474560 | tf_op jit(solution)/shard_map/reduce_scatter | solution.py:304
  405.5 181.2 %reduce-scatter.17.cloned.1.call-start = ((), (), s32[]{:S(2)}) async-start(), calls=%async_computation.21 | async-start | bytes 5898240 | tf_op jit(solution)/shard_map/reduce_scatter | solution.py:331
  412.8 262.0 %reduce-scatter.15.cloned.1.call-start = ((), (), s32[]{:S(2)}) async-start(), calls=%async_computation.20 | async-start | bytes 5898240 | tf_op jit(solution)/shard_map/reduce_scatter | solution.py:325
  420.3 24.9 %copy-start.14 = (bf16[12,64,512]{2,1,0:T(8,128)(2,1)S(1)}, bf16[12,64,512]{2,1,0:T(8,128)(2,1)}, u32[]{:S(2)}) copy-start(bf16[12,64,512]{2,1,0:T(8,128)(2,1)} %copy-done.13) | copy-start | bytes 2359300
  439.6 7.8 copy-start.24
  439.6 30.5 %all-to-all-start.1 = ((bf16[32,16,768]{2,1,0:T(8,128)(2,1)}), bf16[32,16,768]{2,1,0:T(8,128)(2,1)S(1)}, u32[]{:S(2)}, u32[]{:S(2)}) async-start(bf16[32,16,768]{2,1,0:T(8,128)(2,1)} %bitcast.10), calls=%async_computation.1 | async-start | bytes 1572864 | tf_op jit(solution)/shard_map/all_to_all | solution.py:346
  449.4 26.2 %copy-start.38 = (s32[32]{0:T(128)S(1)}, s32[32]{0:T(128)}, u32[]{:S(2)}) copy-start(s32[32]{0:T(128)} %param.24) | copy-start | bytes 388
  470.1 33.2 %all-to-all-start.3 = ((bf16[32,16,768]{2,1,0:T(8,128)(2,1)}), bf16[32,16,768]{2,1,0:T(8,128)(2,1)S(1)}, u32[]{:S(2)}, u32[]{:S(2)}) async-start(bf16[32,16,768]{2,1,0:T(8,128)(2,1)} %bitcast.21), calls=%async_computation.3 | async-start | bytes 1572864 | tf_op jit(solution)/shard_map/all_to_all | solution.py:347
  503.9 315.4 %copy-start.1 = (bf16[512,768]{1,0:T(8,128)(2,1)S(1)}, bf16[512,768]{1,0:T(8,128)(2,1)}, u32[]{:S(2)}) copy-start(bf16[512,768]{1,0:T(8,128)(2,1)} %param.22) | copy-start | bytes 2359300
  (10 other events, 13.4 us)
Sparse Core Ops, SparseCore 0:
  9.6 50.1 all-gather.9
  61.4 40.1 all-gather.11
  103.2 29.4 all-gather.7
  134.0 29.4 all-gather.13
  165.0 88.5 all-gather.15
  255.0 87.7 all-gather.17
  364.1 27.7 reduce-scatter.12
  394.2 27.9 reduce-scatter.10
  424.5 31.1 reduce-scatter.6
  457.9 36.0 reduce-scatter.8
  496.3 90.3 reduce-scatter.16
  588.9 85.7 reduce-scatter.14
where the time goes:
time: 831 us; the launch traced here: 827 us
  waiting for transfers between devices  390 us (47%)
  blocking collectives  260 us (31%)
  matrix products  106 us (13%)
  local copies, waits for them, and re-layouts  22.6 us (3%)
  between operations  18 us (2%)
  other arithmetic  16.4 us (2%)
  starting transfers between devices  14.3 us (2%)
    psum x1, blocking collectives, shards(): totals = lax.psum(tuple(shares), 'rep')  145 us
    reduce_scatter x1, waiting for transfers between devices, shards(): lax.psum_scatter(grad_inner_weight.astype(jnp.bfloat16), 'fsdp', scatter_...  88 us
    all_gather x1, waiting for transfers between devices, shards(): lax.all_gather(inner_weight, 'fsdp', axis=0, tiled=True)  87.1 us
    reduce_scatter x1, waiting for transfers between devices, shards(): lax.psum_scatter(grad_outer_weight.astype(jnp.bfloat16), 'fsdp', scatter_...  81.5 us
    all_gather x1, waiting for transfers between devices, shards(): lax.all_gather(outer_weight, 'fsdp', axis=0, tiled=True)  70 us
    unnamed x2, blocking collectives  57.1 us
    all_to_all x1, blocking collectives, shards(): lax.all_to_all(outgoing(cotangent), ('rep', 'fsdp'), split_axis=0, concat...  44.4 us
    dot_general x6, matrix products, matmul(): return jnp.dot(left, right, preferred_element_type=jnp.float32)  37 us
  transfers between devices with their start and end apart: 15, of which 7 were waited for; matrix products, arithmetic and copies ran while one was open for 14% of the time, Pallas kernels for 0%

commit v1 on v0

--- a/solution.py
+++ b/solution.py
@@ -10,6 +10,19 @@
 masked_score = -1e30
 inv_root_two = 0.7071067811865476
 inv_root_two_pi = 0.3989422804014327
+
+
+def gather_around(x, axis, dim):
+    count, index, rows = (lax.axis_size(axis), lax.axis_index(axis), x.shape[dim])
+    ahead = [(i, (i + 1) % count) for i in range(count)]
+    whole = jnp.zeros((*x.shape[:dim], count * rows, *x.shape[dim + 1 :]), x.dtype)
+    held = x
+    for step in range(count):
+        source = (index - step) % count
+        whole = lax.dynamic_update_slice_in_dim(whole, held, source * rows, axis=dim)
+        if step < count - 1:
+            held = lax.ppermute(held, axis, ahead)
+    return whole
 
 
 def matmul(left, right):
@@ -191,7 +204,7 @@
         lax.all_gather(first_shift, "fsdp", axis=0, tiled=True),
         lax.all_gather(inner_weight, "fsdp", axis=0, tiled=True),
         lax.all_gather(inner_bias, "fsdp", axis=0, tiled=True),
-        lax.all_gather(outer_weight, "fsdp", axis=0, tiled=True),
+        gather_around(outer_weight, "fsdp", 0),
         lax.all_gather(outer_bias, "fsdp", axis=0, tiled=True),
         lax.all_gather(second_gain, "fsdp", axis=0, tiled=True),
         lax.all_gather(second_shift, "fsdp", axis=0, tiled=True),

time: 831 us -> 902 us (1.085)
  waiting for transfers between devices: 390 us -> 480 us
  blocking collectives: 260 us -> 217 us
  starting transfers between devices: 14.3 us -> 24.6 us
    all_to_all x0 -> x1, waiting for transfers between devices: none -> 60.2 us  [shards(): lax.all_to_all(outgoing(cotangent), ('rep', 'fsdp'), split_axis=0, concat...]
    all_to_all x1 -> x0, blocking collectives: 44.4 us -> none  [shards(): lax.all_to_all(outgoing(cotangent), ('rep', 'fsdp'), split_axis=0, concat...]
    ppermute x0 -> x3, waiting for transfers between devices: none -> 33.5 us  [gather_around(): held = lax.ppermute(held, axis, ahead)]
    all_gather x1, waiting for transfers between devices: 87.1 us -> 66.1 us  [shards(): lax.all_gather(inner_weight, 'fsdp', axis=0, tiled=True)]
    dynamic_update_slice x0 -> x4, local copies, waits for them, and re-layouts: none -> 9.81 us  [gather_around(): lax.dynamic_update_slice_in_dim(whole, held, source * rows, axis=dim)]
    all_gather x1, waiting for transfers between devices: 70 us -> 60.2 us  [shards(): lax.all_gather(outer_weight, 'fsdp', axis=0, tiled=True)]
  transfers between devices with their start and end apart: 15 -> 19, of which waited for: 7 -> 12; matrix products, arithmetic and copies ran while one was open for 14% -> 14% of each run, Pallas kernels for 0% -> 0%
where the time goes in v1:
time: 902 us; the launch traced here: 897 us
  waiting for transfers between devices  480 us (53%)
  blocking collectives  217 us (24%)
  matrix products  109 us (12%)
  local copies, waits for them, and re-layouts  30.5 us (3%)
  starting transfers between devices  24.6 us (3%)
  other arithmetic  18.5 us (2%)
  between operations  17.9 us (2%)
    psum x1, blocking collectives, shards(): totals = lax.psum(tuple(shares), 'rep')  145 us
    reduce_scatter x1, waiting for transfers between devices, shards(): lax.psum_scatter(grad_outer_weight.astype(jnp.bfloat16), 'fsdp', scatter_...  88 us
    reduce_scatter x1, waiting for transfers between devices, shards(): lax.psum_scatter(grad_inner_weight.astype(jnp.bfloat16), 'fsdp', scatter_...  86.8 us
    all_gather x1, waiting for transfers between devices, shards(): lax.all_gather(inner_weight, 'fsdp', axis=0, tiled=True)  66.1 us
    all_to_all x1, waiting for transfers between devices, shards(): lax.all_to_all(outgoing(cotangent), ('rep', 'fsdp'), split_axis=0, concat...  60.2 us
    all_gather x1, waiting for transfers between devices, shards(): lax.all_gather(outer_weight, 'fsdp', axis=0, tiled=True)  60.2 us
    unnamed x2, blocking collectives  58.4 us
    dot_general x6, matrix products, matmul(): return jnp.dot(left, right, preferred_element_type=jnp.float32)  37.2 us
  transfers between devices with their start and end apart: 19, of which 12 were waited for; matrix products, arithmetic and copies ran while one was open for 14% of the time, Pallas kernels for 0%

profile of v1, /device:TPU:0, one launch (start us, length us, event | category | flops | bytes accessed | tf_op | source)
XLA Modules:
  0.0 896.9 jit_solution(563433852443564842)
XLA Ops:
  14.1 7.3 all-to-all-start.2
  23.2 60.2 %all-to-all-done.2 = bf16[32,16,768]{2,1,0:T(8,128)(2,1)S(1)} async-done(((bf16[32,16,768]{2,1,0:T(8,128)(2,1)}), bf16[32,16,768]{2,1,0:T(8,128)(2,1)S(1)}, u32[]{:S(2)}, u32[]{:S(2)}) %all-to-all-start.2) | async-done | bytes 786464 | tf_op jit(solution)/shard_map/all_to_all | solution.py:174
  83.4 3.7 all-to-all-start
  90.8 41.5 %all-reduce.19 = (bf16[768]{0:T(1024)(128)(2,1)S(1)}, bf16[768]{0:T(1024)(128)(2,1)S(1)}, bf16[768]{0:T(1024)(128)(2,1)S(1)}, bf16[768]{0:T(1024)(128)(2,1)S(1)}...) all-reduce(bf16[768]{0:T(1024)(128)(2,1)S(1)} %dynamic-update-slice, ...), channel_id=1, replica_groups=mesh['rep'=8,'fsdp'=4] {'fsdp'}, use_global_device_ids=true, to_apply=%add | all-reduce | flops 5376 | bytes 21504
  133.0 13.5 %all-gather = bf16[4,1,768]{2,1,0:T(2,128)(2,1)S(1)} all-gather(bf16[1,1,768]{2,1,0:T(2,128)(2,1)S(1)} %reshape.251), channel_id=1, replica_groups=mesh['rep'=8,'fsdp'=4] {'fsdp'}, dimensions={0}, use_global_device_ids=true | all-gather | bytes 7680 | tf_op jit(solution)/shard_map/all_gather | solution.py:206
  146.6 2.4 broadcast_in_dim.117
  149.0 2.4 constant_dynamic-update-slice_fusion.3
  151.9 2.4 constant_dynamic-update-slice_fusion.2
  154.9 2.3 add_convert_fusion.1
  157.6 3.2 convolution_convert_fusion.7
  162.2 2.6 all-gather.8.cloned.1.call-done
  164.8 2.9 add_convert_fusion.2
  169.1 3.0 fusion.37
  174.0 2.7 copy-done.2
  176.7 3.2 fusion.27
  179.9 12.9 %collective-permute-done.1 = bf16[768,768]{1,0:T(8,128)(2,1)} collective-permute-done((bf16[768,768]{1,0:T(8,128)(2,1)}, bf16[768,768]{1,0:T(8,128)(2,1)}, u32[]{:S(2)}, u32[]{:S(2)}) %collective-permute-start.1) | collective-permute-done | bytes 1179680 | tf_op jit(solution)/shard_map/ppermute | solution.py:24
  192.8 2.8 collective-permute-start.2
  195.6 14.8 %all-gather.14.cloned.1.call-done = bf16[768,768]{1,0:T(8,128)(2,1)} async-done(((bf16[192,768]{1,0:T(8,128)(2,1)}), bf16[768,768]{1,0:T(8,128)(2,1)}) %all-gather.14.cloned.1.call-update) | async-done | bytes 1179664 | tf_op jit(solution)/shard_map/all_gather | solution.py:201
  210.5 2.6 fusion.38
  213.5 2.6 constant_dynamic-update-slice_fusion.1
  216.1 20.6 %collective-permute-done.2 = bf16[768,768]{1,0:T(8,128)(2,1)} collective-permute-done((bf16[768,768]{1,0:T(8,128)(2,1)}, bf16[768,768]{1,0:T(8,128)(2,1)}, u32[]{:S(2)}, u32[]{:S(2)}) %collective-permute-start.2) | collective-permute-done | bytes 1179680 | tf_op jit(solution)/shard_map/ppermute | solution.py:24
  236.7 2.4 constant_dynamic-update-slice_fusion
  239.1 66.1 %all-gather.16.cloned.1.call-done = bf16[768,3072]{1,0:T(8,128)(2,1)} async-done(((bf16[192,3072]{1,0:T(8,128)(2,1)}), bf16[768,3072]{1,0:T(8,128)(2,1)}) %all-gather.16.cloned.1.call-update) | async-done | bytes 4718608 | tf_op jit(solution)/shard_map/all_gather | solution.py:205
  305.2 19.3 %fusion.4 = (bf16[512,3072]{1,0:T(8,128)(2,1)S(1)}, f32[512,3072]{1,0:T(8,128)}) fusion(f32[3072]{0:T(1024)S(1)} %bitcast.109, bf16[768,3072]{1,0:T(8,128)(2,1)} %all-gather.16.cloned.1.call-done, f32[512,768]{1,0:T(8,128)S(1)} %get-tuple-element.122, f32[768]{0:T(1024)S(1)} %convert_element_type.228, f32[768]{0:T(1024)S(1)} %convert_element_type.227, ...), kind=kOutput, calls=%fused_computation.16 | convolution fusion | flops 2521694208 | bytes 15751168 | tf_op jit(solution)/shard_map/dot_general | solution.py:29
  324.5 6.8 fusion.39
  334.0 60.2 %all-gather.18.cloned.1.call-done = bf16[3072,768]{1,0:T(8,128)(2,1)} async-done(((bf16[768,768]{1,0:T(8,128)(2,1)}), bf16[3072,768]{1,0:T(8,128)(2,1)}) %all-gather.18.cloned.1.call-update) | async-done | bytes 4718608 | tf_op jit(solution)/shard_map/all_gather | solution.py:257
  394.2 7.9 fusion.40
  402.2 6.6 multiply_reduce_fusion.2
  413.7 6.8 bitcast_reduce_fusion
  421.4 1.9 convolution_convert_fusion.3
  423.3 6.9 multiply_reduce_fusion
  430.3 6.8 multiply_convert_fusion
  442.6 4.9 multiply_convert_fusion.1
  448.4 1.9 convolution_convert_fusion.4
  450.3 3.2 convolution_convert_fusion.2
  453.6 7.4 convolution_convert_fusion.1
  461.3 7.2 convolution_convert_fusion
  469.5 16.9 %all-reduce.18 = (bf16[768]{0:T(1024)(128)(2,1)S(1)}, bf16[768]{0:T(1024)(128)(2,1)S(1)}, bf16[768]{0:T(1024)(128)(2,1)S(1)}, bf16[768]{0:T(1024)(128)(2,1)S(1)}...) all-reduce(bf16[768]{0:T(1024)(128)(2,1)S(1)} %dynamic-update-slice, ...), channel_id=1, replica_groups=mesh['rep'=8,'fsdp'=4] {'fsdp'}, use_global_device_ids=true, to_apply=%add.7 | all-reduce | flops 9984 | bytes 39936
  488.0 4.0 all-to-all-start.1
  493.3 2.2 fusion.41
  495.6 2.1 fusion.42
  499.4 27.8 %all-to-all-done.1 = bf16[32,16,768]{2,1,0:T(8,128)(2,1)S(1)} async-done(((bf16[32,16,768]{2,1,0:T(8,128)(2,1)}), bf16[32,16,768]{2,1,0:T(8,128)(2,1)S(1)}, u32[]{:S(2)}, u32[]{:S(2)}) %all-to-all-start.1) | async-done | bytes 786464 | tf_op jit(solution)/shard_map/all_to_all | solution.py:359
  527.2 3.7 all-to-all-start.3
  532.3 31.8 %all-to-all-done.3 = bf16[32,16,768]{2,1,0:T(8,128)(2,1)S(1)} async-done(((bf16[32,16,768]{2,1,0:T(8,128)(2,1)}), bf16[32,16,768]{2,1,0:T(8,128)(2,1)S(1)}, u32[]{:S(2)}, u32[]{:S(2)}) %all-to-all-start.3) | async-done | bytes 786464 | tf_op jit(solution)/shard_map/all_to_all | solution.py:360
  566.1 4.5 reduce-scatter.13.cloned.1.call-done
  570.5 86.8 %reduce-scatter.15.cloned.1.call-done = bf16[192,3072]{1,0:T(8,128)(2,1)} async-done(((bf16[768,3072]{1,0:T(8,128)(2,1)}), bf16[192,3072]{1,0:T(8,128)(2,1)}) %reduce-scatter.15.cloned.1.call-update) | async-done | bytes 1179664 | tf_op jit(solution)/shard_map/reduce_scatter | solution.py:338
  657.3 88.0 %reduce-scatter.17.cloned.1.call-done = bf16[768,768]{1,0:T(8,128)(2,1)} async-done(((bf16[3072,768]{1,0:T(8,128)(2,1)}), bf16[768,768]{1,0:T(8,128)(2,1)}) %reduce-scatter.17.cloned.1.call-update) | async-done | bytes 1179664 | tf_op jit(solution)/shard_map/reduce_scatter | solution.py:344
  745.3 144.6 %all-reduce.21 = (f32[192,768]{1,0:T(8,128)}, f32[192]{0:T(256)}, f32[192,768]{1,0:T(8,128)}, f32[192,768]{1,0:T(8,128)}, f32[192]{0:T(256)}, /*index=5*/f32[192...) all-reduce(bf16[192,768]{1,0:T(8,128)(2,1)} %reduce-scatter.7.clone, ...), channel_id=1, replica_groups=mesh['rep'=8,'fsdp'=4] {'rep'}, use_global_device_ids=true, to_apply=%region_13.15 | all-reduce | flops 1771776 | bytes 10635264 | tf_op jit(solution)/shard_map/psum | solution.py:357
  (188 shorter events, 40.5 us)
Async XLA Ops:
  7.2 4.2 copy-start
  7.2 4.8 copy-start.18
  7.2 147.7 %all-gather.10.cloned.1.call-start = ((), (), s32[]{:S(2)}) async-start(), calls=%async_computation.11 | async-start | bytes 1474560 | tf_op jit(solution)/shard_map/all_gather | solution.py:196
  8.0 149.6 %all-gather.12.cloned.1.call-start = ((), (), s32[]{:S(2)}) async-start(), calls=%async_computation.12 | async-start | bytes 1474560 | tf_op jit(solution)/shard_map/all_gather | solution.py:198
  8.7 156.1 %all-gather.8.cloned.1.call-start = ((), (), s32[]{:S(2)}) async-start(), calls=%async_computation.10 | async-start | bytes 1474560 | tf_op jit(solution)/shard_map/all_gather | solution.py:199
  9.4 201.0 %all-gather.14.cloned.1.call-start = ((), (), s32[]{:S(2)}) async-start(), calls=%async_computation.13 | async-start | bytes 1474560 | tf_op jit(solution)/shard_map/all_gather | solution.py:201
  10.0 295.2 %all-gather.16.cloned.1.call-start = ((), (), s32[]{:S(2)}) async-start(), calls=%async_computation.14 | async-start | bytes 5898240 | tf_op jit(solution)/shard_map/all_gather | solution.py:205
  12.6 75.2 %copy-start.25 = (u32[32]{0:T(128)S(1)}, u32[32]{0:T(128)}, u32[]{:S(2)}) copy-start(u32[32]{0:T(128)} %constant.182) | copy-start | bytes 388
  12.6 76.5 %copy-start.28 = (bf16[192]{0:T(256)(128)(2,1)S(1)}, bf16[192]{0:T(256)(128)(2,1)}, u32[]{:S(2)}) copy-start(bf16[192]{0:T(256)(128)(2,1)} %param.29) | copy-start | bytes 1156
  12.7 76.7 %copy-start.29 = (bf16[192]{0:T(256)(128)(2,1)S(1)}, bf16[192]{0:T(256)(128)(2,1)}, u32[]{:S(2)}) copy-start(bf16[192]{0:T(256)(128)(2,1)} %param.26) | copy-start | bytes 1156
  12.7 76.9 %copy-start.30 = (bf16[192]{0:T(256)(128)(2,1)S(1)}, bf16[192]{0:T(256)(128)(2,1)}, u32[]{:S(2)}) copy-start(bf16[192]{0:T(256)(128)(2,1)} %param.31) | copy-start | bytes 1156
  12.7 77.1 %copy-start.31 = (bf16[192]{0:T(256)(128)(2,1)S(1)}, bf16[192]{0:T(256)(128)(2,1)}, u32[]{:S(2)}) copy-start(bf16[192]{0:T(256)(128)(2,1)} %param.32) | copy-start | bytes 1156
  12.7 77.4 %copy-start.32 = (bf16[192]{0:T(256)(128)(2,1)S(1)}, bf16[192]{0:T(256)(128)(2,1)}, u32[]{:S(2)}) copy-start(bf16[192]{0:T(256)(128)(2,1)} %param.33) | copy-start | bytes 1156
  12.7 77.6 %copy-start.33 = (bf16[192]{0:T(256)(128)(2,1)S(1)}, bf16[192]{0:T(256)(128)(2,1)}, u32[]{:S(2)}) copy-start(bf16[192]{0:T(256)(128)(2,1)} %param.37) | copy-start | bytes 1156
  12.7 77.8 %copy-start.34 = (bf16[192]{0:T(256)(128)(2,1)S(1)}, bf16[192]{0:T(256)(128)(2,1)}, u32[]{:S(2)}) copy-start(bf16[192]{0:T(256)(128)(2,1)} %param.38) | copy-start | bytes 1156
  12.7 120.2 %copy-start.26 = (bf16[768]{0:T(1024)(128)(2,1)S(1)}, bf16[768]{0:T(1024)(128)(2,1)}, u32[]{:S(2)}) copy-start(bf16[768]{0:T(1024)(128)(2,1)} %param.35) | copy-start | bytes 4612
  14.1 69.3 %all-to-all-start.2 = ((bf16[32,16,768]{2,1,0:T(8,128)(2,1)}), bf16[32,16,768]{2,1,0:T(8,128)(2,1)S(1)}, u32[]{:S(2)}, u32[]{:S(2)}) async-start(bf16[32,16,768]{2,1,0:T(8,128)(2,1)} %get-tuple-element.117), calls=%async_computation.2 | async-start | bytes 1572864 | tf_op jit(solution)/shard_map/all_to_all | solution.py:174
  21.4 130.0 %collective-permute-start = (bf16[768,768]{1,0:T(8,128)(2,1)}, bf16[768,768]{1,0:T(8,128)(2,1)}, u32[]{:S(2)}, u32[]{:S(2)}) collective-permute-start(bf16[768,768]{1,0:T(8,128)(2,1)} %param.36), channel_id=1, source_target_pairs={{0,1},{1,2},{2,3},{3,0},{4,5},{5,6},{6,7},{7,4},{8,9},{9,10},{10,1... | collective-permute-start | bytes 3538952 | tf_op jit(solution)/shard_map/ppermute | solution.py:24
  83.4 71.4 %all-to-all-start = ((bf16[32,16,768]{2,1,0:T(8,128)(2,1)}), bf16[32,16,768]{2,1,0:T(8,128)(2,1)S(1)}, u32[]{:S(2)}, u32[]{:S(2)}) async-start(bf16[32,16,768]{2,1,0:T(8,128)(2,1)} %get-tuple-element.118), calls=%async_computation | async-start | bytes 1572864 | tf_op jit(solution)/shard_map/all_to_all | solution.py:173
  87.1 307.1 %all-gather.18.cloned.1.call-start = ((), (), s32[]{:S(2)}) async-start(), calls=%async_computation.15 | async-start | bytes 5898240 | tf_op jit(solution)/shard_map/all_gather | solution.py:257
  87.7 478.3 %reduce-scatter.11.cloned.1.call-start = ((), (), s32[]{:S(2)}) async-start(), calls=%async_computation.18 | async-start | bytes 1474560 | tf_op jit(solution)/shard_map/reduce_scatter | solution.py:320
  151.4 41.4 %collective-permute-start.1 = (bf16[768,768]{1,0:T(8,128)(2,1)}, bf16[768,768]{1,0:T(8,128)(2,1)}, u32[]{:S(2)}, u32[]{:S(2)}) collective-permute-start(bf16[768,768]{1,0:T(8,128)(2,1)} %collective-permute-done), channel_id=1, source_target_pairs={{0,1},{1,2},{2,3},{3,0},{4,5},{5,6},{6,7},{7,4},{8,9},{9,10},{10,1... | collective-permute-start | bytes 3538952 | tf_op jit(solution)/shard_map/ppermute | solution.py:24
  154.9 9.9 %copy-start.19 = (bf16[32,16,768]{2,1,0:T(8,128)(2,1)}, bf16[32,16,768]{2,1,0:T(8,128)(2,1)S(1)}, u32[]{:S(2)}) copy-start(bf16[32,16,768]{2,1,0:T(8,128)(2,1)S(1)} %all-to-all-done) | copy-start | bytes 2359300
  157.5 11.6 %copy-start.6 = (bf16[512,768]{0,1:T(8,128)(2,1)}, bf16[512,768]{0,1:T(8,128)(2,1)S(1)}, u32[]{:S(2)}) copy-start(bf16[512,768]{0,1:T(8,128)(2,1)S(1)} %copy.65) | copy-start | bytes 2359300
  169.1 4.9 copy-start.10
  172.2 4.5 copy-start.2
  192.8 43.9 %collective-permute-start.2 = (bf16[768,768]{1,0:T(8,128)(2,1)}, bf16[768,768]{1,0:T(8,128)(2,1)}, u32[]{:S(2)}, u32[]{:S(2)}) collective-permute-start(bf16[768,768]{1,0:T(8,128)(2,1)} %collective-permute-done.1), channel_id=1, source_target_pairs={{0,1},{1,2},{2,3},{3,0},{4,5},{5,6},{6,7},{7,4},{8,9},{9,10},{10,1... | collective-permute-start | bytes 3538952 | tf_op jit(solution)/shard_map/ppermute | solution.py:24
  213.1 92.1 %copy-start.8 = (f32[512,768]{1,0:T(8,128)}, f32[512,768]{1,0:T(8,128)S(1)}, u32[]{:S(2)}) copy-start(f32[512,768]{1,0:T(8,128)S(1)} %get-tuple-element.122) | copy-start | bytes 4718596
  324.5 6.8 copy-start.37
  394.2 8.0 copy-start.9
  394.2 8.0 copy-start.15
  402.2 6.6 copy-start.38
  413.7 7.7 copy-start.20
  423.3 142.8 %reduce-scatter.7.cloned.1.call-start = ((), (), s32[]{:S(2)}) async-start(), calls=%async_computation.16 | async-start | bytes 1474560 | tf_op jit(solution)/shard_map/reduce_scatter | solution.py:311
  442.6 5.8 copy-start.22
  442.6 123.5 %reduce-scatter.9.cloned.1.call-start = ((), (), s32[]{:S(2)}) async-start(), calls=%async_computation.17 | async-start | bytes 1474560 | tf_op jit(solution)/shard_map/reduce_scatter | solution.py:317
  450.3 120.3 %reduce-scatter.13.cloned.1.call-start = ((), (), s32[]{:S(2)}) async-start(), calls=%async_computation.19 | async-start | bytes 1474560 | tf_op jit(solution)/shard_map/reduce_scatter | solution.py:326
  453.6 203.7 %reduce-scatter.15.cloned.1.call-start = ((), (), s32[]{:S(2)}) async-start(), calls=%async_computation.20 | async-start | bytes 5898240 | tf_op jit(solution)/shard_map/reduce_scatter | solution.py:338
  461.0 284.2 %reduce-scatter.17.cloned.1.call-start = ((), (), s32[]{:S(2)}) async-start(), calls=%async_computation.21 | async-start | bytes 5898240 | tf_op jit(solution)/shard_map/reduce_scatter | solution.py:344
  468.5 24.8 %copy-start.14 = (bf16[12,64,512]{2,1,0:T(8,128)(2,1)S(1)}, bf16[12,64,512]{2,1,0:T(8,128)(2,1)}, u32[]{:S(2)}) copy-start(bf16[12,64,512]{2,1,0:T(8,128)(2,1)} %copy-done.13) | copy-start | bytes 2359300
  488.0 7.6 copy-start.24
  488.0 39.2 %all-to-all-start.1 = ((bf16[32,16,768]{2,1,0:T(8,128)(2,1)}), bf16[32,16,768]{2,1,0:T(8,128)(2,1)S(1)}, u32[]{:S(2)}, u32[]{:S(2)}) async-start(bf16[32,16,768]{2,1,0:T(8,128)(2,1)} %bitcast.10), calls=%async_computation.1 | async-start | bytes 1572864 | tf_op jit(solution)/shard_map/all_to_all | solution.py:359
  493.3 4.4 copy-start.5
  493.3 4.4 copy-start.12
  493.3 4.4 copy-start.16
  497.7 33.2 %copy-start.36 = (s32[32]{0:T(128)S(1)}, s32[32]{0:T(128)}, u32[]{:S(2)}) copy-start(s32[32]{0:T(128)} %param.24) | copy-start | bytes 388
  527.2 36.9 %all-to-all-start.3 = ((bf16[32,16,768]{2,1,0:T(8,128)(2,1)}), bf16[32,16,768]{2,1,0:T(8,128)(2,1)S(1)}, u32[]{:S(2)}, u32[]{:S(2)}) async-start(bf16[32,16,768]{2,1,0:T(8,128)(2,1)} %bitcast.21), calls=%async_computation.3 | async-start | bytes 1572864 | tf_op jit(solution)/shard_map/all_to_all | solution.py:360
  564.1 325.8 %copy-start.1 = (bf16[512,768]{1,0:T(8,128)(2,1)S(1)}, bf16[512,768]{1,0:T(8,128)(2,1)}, u32[]{:S(2)}) copy-start(bf16[512,768]{1,0:T(8,128)(2,1)} %param.21) | copy-start | bytes 2359300
  (10 other events, 18.1 us)
Sparse Core Ops, SparseCore 0:
  9.6 75.4 all-gather.9
  86.6 40.6 all-gather.11
  128.9 35.7 all-gather.7
  166.2 44.2 all-gather.13
  211.9 93.2 all-gather.15
  306.6 87.5 all-gather.17
  423.4 27.7 reduce-scatter.10
  453.5 28.6 reduce-scatter.6
  484.5 40.5 reduce-scatter.8
  527.2 43.2 reduce-scatter.12
  572.8 84.4 reduce-scatter.14
  659.5 85.7 reduce-scatter.16
